TPU v7x, 32 devices: a whole 2x2x4 slice. The times are simulated.
32 devices in a mesh: dp: 8 (over z, y), tensor: 4 (over x, core).
Axes of the slice: x: 2, y: 2, z: 4, core: 2. Of those that a mesh axis runs over, the one named last changes fastest.
Arguments:
- tokens: bfloat16 [37632, 768], P(('dp', 'tensor')), may hold values from -21 to 21
- res_class: int32 [192], P('dp'), may hold values from 0 to 1
- gain_attn: float32 [768], replicated, may hold values from 0.5 to 1.5
- shift_attn: float32 [768], replicated, may hold values from -1.5 to 1.5
- w_qkv: bfloat16 [768, 3, 768], P(None, None, 'tensor'), may hold values from -0.3125 to 0.3125
- bias_qv: float32 [2, 768], P(None, 'tensor'), may hold values from -1.5 to 1.5
- w_out: bfloat16 [768, 768], P('tensor'), may hold values from -0.625 to 0.625
- bias_out: float32 [768], replicated, may hold values from -1.5 to 1.5
- gain_mlp: float32 [768], replicated, may hold values from 0.5 to 1.5
- shift_mlp: float32 [768], replicated, may hold values from -1.5 to 1.5
- w_up: bfloat16 [768, 3072], P(None, 'tensor'), may hold values from -0.21875 to 0.21875
- bias_up: float32 [3072], P('tensor'), may hold values from -1.5 to 1.5
- w_down: bfloat16 [3072, 768], P('tensor'), may hold values from -0.15625 to 0.15625
- bias_down: float32 [768], replicated, may hold values from -1.5 to 1.5
- cotangent: bfloat16 [37632, 768], P(('dp', 'tensor')), may hold values from -21 to 21
Outputs:
- block_out: bfloat16 [37632, 768], P(('dp', 'tensor'))
- grad_tokens: float32 [37632, 768], P(('dp', 'tensor'))
- grad_gain_attn: float32 [768], replicated
- grad_shift_attn: float32 [768], replicated
- grad_qkv: float32 [768, 3, 768], P(None, None, 'tensor')
- grad_bias_qv: float32 [2, 768], P(None, 'tensor')
- grad_out: float32 [768, 768], P('tensor')
- grad_bias_out: float32 [768], replicated
- grad_gain_mlp: float32 [768], replicated
- grad_shift_mlp: float32 [768], replicated
- grad_up: float32 [768, 3072], P(None, 'tensor')
- grad_bias_up: float32 [3072], P('tensor')
- grad_down: float32 [3072, 768], P('tensor')
- grad_bias_down: float32 [768], replicated
- rms: float32 [3], replicated
All inputs are finite; a program needn't handle non-finite values.
Results may differ from a plain program's by a relative error of at most 0.017.
Values may be sent and summed in bfloat16 or wider, within the bound.
A program may use at most 256 MiB of HBM per device.

v0:
```python
import jax
import jax.numpy as jnp
from jax import lax
from jax.sharding import PartitionSpec as P

HEAD_DIM = 64
PATCHES = 196
PATCHES_LOW = 144
EPS = 1e-06


def normalize(values):
    mean = jnp.mean(values, axis=-1, keepdims=True)
    centred = values - mean
    factor = lax.rsqrt(jnp.mean(centred * centred, axis=-1, keepdims=True) + EPS)
    return (centred * factor, factor)


def norm_back(grad_out, gain, normed, factor):
    scaled = grad_out * gain
    return factor * (
        scaled
        - jnp.mean(scaled, axis=-1, keepdims=True)
        - normed * jnp.mean(scaled * normed, axis=-1, keepdims=True)
    )


def exact_gelu(values):
    return jax.nn.gelu(values, approximate=False)


def on_device(
    tokens,
    res_class,
    gain_attn,
    shift_attn,
    w_qkv,
    bias_qv,
    w_out,
    bias_out,
    gain_mlp,
    shift_mlp,
    w_up,
    bias_up,
    w_down,
    bias_down,
    cotangent,
):
    rows = tokens.shape[0]
    width = tokens.shape[1]
    images = res_class.shape[0]
    local = w_qkv.shape[2]
    heads_here = local // HEAD_DIM
    scale = HEAD_DIM ** (-0.5)
    place = lax.axis_index("tensor")
    counts = jnp.where(res_class == 0, PATCHES, PATCHES_LOW)
    key_valid = jnp.arange(PATCHES)[None, :] < counts[:, None]
    flat_valid = key_valid.reshape(-1).astype(jnp.float32)
    row_valid = lax.dynamic_slice_in_dim(flat_valid, place * rows, rows)[:, None]
    mask = key_valid[:, None, None, :]
    shape = (images, PATCHES, heads_here, HEAD_DIM)
    w_qkv_flat = w_qkv.reshape(width, 3 * local)
    inputs = tokens.astype(jnp.float32)
    normed_a, factor_a = normalize(inputs)
    in_attn = (normed_a * gain_attn + shift_attn).astype(jnp.bfloat16)
    full_attn = lax.all_gather(in_attn, "tensor", axis=0, tiled=True)
    qkv = jnp.dot(full_attn, w_qkv_flat, preferred_element_type=jnp.float32).reshape(-1, 3, local)
    query = (qkv[:, 0] + bias_qv[0]).astype(jnp.bfloat16).reshape(shape)
    keys = qkv[:, 1].astype(jnp.bfloat16).reshape(shape)
    values = (qkv[:, 2] + bias_qv[1]).astype(jnp.bfloat16).reshape(shape)
    scores = jnp.einsum("iqhd,ikhd->ihqk", query, keys, preferred_element_type=jnp.float32) * scale
    scores = jnp.where(mask, scores, -1e30)
    log_total = jax.nn.logsumexp(scores, axis=-1, keepdims=True)
    probs = jnp.exp(scores - log_total).astype(jnp.bfloat16)
    context = (
        jnp.einsum("ihqk,ikhd->iqhd", probs, values, preferred_element_type=jnp.float32)
        .reshape(-1, local)
        .astype(jnp.bfloat16)
    )
    piece = context
    branch = (
        lax.psum_scatter(
            jnp.dot(piece, w_out, preferred_element_type=jnp.float32).astype(jnp.bfloat16),
            "tensor",
            scatter_dimension=0,
            tiled=True,
        ).astype(jnp.float32)
        + bias_out
    )
    hidden = inputs + branch
    normed_m, factor_m = normalize(hidden)
    in_mlp = (normed_m * gain_mlp + shift_mlp).astype(jnp.bfloat16)
    full_mlp = lax.all_gather(in_mlp, "tensor", axis=0, tiled=True)
    pre_act = jnp.dot(full_mlp, w_up, preferred_element_type=jnp.float32) + bias_up
    act = exact_gelu(pre_act).astype(jnp.bfloat16)
    piece = act
    mlp = (
        lax.psum_scatter(
            jnp.dot(piece, w_down, preferred_element_type=jnp.float32).astype(jnp.bfloat16),
            "tensor",
            scatter_dimension=0,
            tiled=True,
        ).astype(jnp.float32)
        + bias_down
    )
    stream = (hidden + mlp) * row_valid
    block_out = stream.astype(jnp.bfloat16)
    grad_stream = cotangent.astype(jnp.float32) * row_valid
    grad_bias_down = jnp.sum(grad_stream, axis=0)
    grad_mlp_full = lax.all_gather(grad_stream.astype(jnp.bfloat16), "tensor", axis=0, tiled=True)
    weight_down = jnp.einsum("tf,td->fd", act, grad_mlp_full, preferred_element_type=jnp.float32)
    grad_act = jnp.einsum("td,fd->tf", grad_mlp_full, w_down, preferred_element_type=jnp.float32)
    gelu_out, gelu_back = jax.vjp(exact_gelu, pre_act)
    grad_pre = gelu_back(grad_act)[0]
    grad_bias_up = jnp.sum(grad_pre, axis=0)
    grad_pre_low = grad_pre.astype(jnp.bfloat16)
    weight_up = jnp.einsum("td,tf->df", full_mlp, grad_pre_low, preferred_element_type=jnp.float32)
    piece = grad_pre_low
    grad_in_mlp = lax.psum_scatter(
        jnp.einsum("tf,df->td", piece, w_up, preferred_element_type=jnp.float32).astype(
            jnp.bfloat16
        ),
        "tensor",
        scatter_dimension=0,
        tiled=True,
    ).astype(jnp.float32)
    grad_gain_mlp = jnp.sum(grad_in_mlp * normed_m, axis=0)
    grad_shift_mlp = jnp.sum(grad_in_mlp, axis=0)
    grad_hidden = grad_stream + norm_back(grad_in_mlp, gain_mlp, normed_m, factor_m)
    grad_bias_out = jnp.sum(grad_hidden, axis=0)
    grad_branch_full = lax.all_gather(
        grad_hidden.astype(jnp.bfloat16), "tensor", axis=0, tiled=True
    )
    weight_out = jnp.einsum(
        "tc,td->cd", context, grad_branch_full, preferred_element_type=jnp.float32
    )
    grad_context = (
        jnp.einsum("td,cd->tc", grad_branch_full, w_out, preferred_element_type=jnp.float32)
        .astype(jnp.bfloat16)
        .reshape(shape)
    )
    again = jnp.einsum("iqhd,ikhd->ihqk", query, keys, preferred_element_type=jnp.float32) * scale
    again = jnp.where(mask, again, -1e30)
    probs_full = jnp.exp(again - log_total)
    probs_low = probs_full.astype(jnp.bfloat16)
    grad_value = jnp.einsum(
        "ihqk,iqhd->ikhd", probs_low, grad_context, preferred_element_type=jnp.float32
    )
    grad_probs = jnp.einsum(
        "iqhd,ikhd->ihqk", grad_context, values, preferred_element_type=jnp.float32
    )
    row_dot = jnp.sum(probs_full * grad_probs, axis=-1, keepdims=True)
    grad_scores = (probs_full * (grad_probs - row_dot)).astype(jnp.bfloat16)
    grad_query = scale * jnp.einsum(
        "ihqk,ikhd->iqhd", grad_scores, keys, preferred_element_type=jnp.float32
    )
    grad_key = scale * jnp.einsum(
        "ihqk,iqhd->ikhd", grad_scores, query, preferred_element_type=jnp.float32
    )
    query_low = grad_query.reshape(-1, local).astype(jnp.bfloat16)
    key_low = grad_key.reshape(-1, local).astype(jnp.bfloat16)
    value_low = grad_value.reshape(-1, local).astype(jnp.bfloat16)
    grad_bias_qv = jnp.stack(
        [
            jnp.sum(query_low.astype(jnp.float32), axis=0),
            jnp.sum(value_low.astype(jnp.float32), axis=0),
        ]
    )
    grad_qkv_low = jnp.stack([query_low, key_low, value_low], axis=1).reshape(-1, 3 * local)
    weight_qkv = jnp.einsum(
        "td,tc->dc", full_attn, grad_qkv_low, preferred_element_type=jnp.float32
    ).reshape(width, 3, local)
    piece = grad_qkv_low
    grad_in_attn = lax.psum_scatter(
        jnp.einsum("tc,dc->td", piece, w_qkv_flat, preferred_element_type=jnp.float32).astype(
            jnp.bfloat16
        ),
        "tensor",
        scatter_dimension=0,
        tiled=True,
    ).astype(jnp.float32)
    grad_gain_attn = jnp.sum(grad_in_attn * normed_a, axis=0)
    grad_shift_attn = jnp.sum(grad_in_attn, axis=0)
    grad_tokens = grad_hidden + norm_back(grad_in_attn, gain_attn, normed_a, factor_a)
    totals = jnp.stack(
        [
            jnp.sum(stream * stream),
            jnp.sum(branch * branch * row_valid),
            jnp.sum(mlp * mlp * row_valid),
            jnp.sum(row_valid),
        ]
    )
    summed = lax.psum(
        (
            grad_gain_attn,
            grad_shift_attn,
            grad_bias_out,
            grad_gain_mlp,
            grad_shift_mlp,
            grad_bias_down,
            totals,
        ),
        ("dp", "tensor"),
    )
    weight_qkv, grad_bias_qv, weight_out, weight_up, grad_bias_up, weight_down = lax.psum(
        (weight_qkv, grad_bias_qv, weight_out, weight_up, grad_bias_up, weight_down), "dp"
    )
    sums = summed[6]
    rms = jnp.sqrt(sums[:3] / (sums[3] * width))
    return (
        block_out,
        grad_tokens,
        summed[0],
        summed[1],
        weight_qkv,
        grad_bias_qv,
        weight_out,
        summed[2],
        summed[3],
        summed[4],
        weight_up,
        grad_bias_up,
        weight_down,
        summed[5],
        rms,
    )


def solution(mesh):
    in_specs = (
        P(("dp", "tensor"), None),
        P("dp"),
        P(),
        P(),
        P(None, None, "tensor"),
        P(None, "tensor"),
        P("tensor", None),
        P(),
        P(),
        P(),
        P(None, "tensor"),
        P("tensor"),
        P("tensor", None),
        P(),
        P(("dp", "tensor"), None),
    )
    out_specs = (
        P(("dp", "tensor"), None),
        P(("dp", "tensor"), None),
        P(),
        P(),
        P(None, None, "tensor"),
        P(None, "tensor"),
        P("tensor", None),
        P(),
        P(),
        P(),
        P(None, "tensor"),
        P("tensor"),
        P("tensor", None),
        P(),
        P(),
    )
    return jax.shard_map(
        on_device, mesh=mesh, in_specs=in_specs, out_specs=out_specs, check_vma=False
    )
```

profile of v0, /device:TPU:0, one launch (start us, length us, event | category | flops | bytes accessed | tf_op | source)
XLA Modules:
  0.0 985.3 jit_solution(16900257428672392909)
XLA Ops:
  16.8 52.4 %all-gather.5.cloned.1.call-done = bf16[4704,768]{1,0:T(8,128)(2,1)} async-done(((bf16[1176,768]{1,0:T(8,128)(2,1)}), bf16[4704,768]{1,0:T(8,128)(2,1)}) %all-gather.5.cloned.1.call-update) | async-done | bytes 7225360 | tf_op jit(solution)/shard_map/all_gather | solution.py:66
  69.2 7.3 fusion.10
  77.9 3.4 fusion.73
  81.4 6.0 convert_element_type.155
  87.4 6.4 squeeze.9
  93.9 6.4 squeeze.8
  100.3 7.4 fusion.6
  108.3 4.7 exponential_reduce_fusion
  114.0 11.1 %convert_bitcast_fusion = bf16[24,196,3,64]{1,3,2,0:T(8,128)(2,1)S(1)} fusion(f32[24,196,3,64]{1,0,3,2:T(8,128)} %squeeze.8, f32[3,64]{1,0:T(4,128)} %add.138, f32[24,3,196,196]{2,3,1,0:T(8,128)} %copy-done.2, f32[24,3,196]{2,1,0:T(4,128)S(1)} %log_add_fusion, pred[24,196]{1,0:T(8,128)(4,1)S(1)} %get-tuple-element.54), kind=kOutput, calls=%fused_computation.91 | convolution fusion | flops 367815168 | bytes 16544736 | tf_op jit(solution)/shard_map/ihqk,ikhd->iqhd/dot_general | solution.py:76
  127.9 4.7 convert_element_type.159
  132.6 6.5 convolution_convert_fusion.2
  140.7 63.8 %reduce-scatter.5.cloned.1.call-done = bf16[1176,768]{1,0:T(8,128)(2,1)} async-done(((bf16[4704,768]{1,0:T(8,128)(2,1)}), bf16[1176,768]{1,0:T(8,128)(2,1)}) %reduce-scatter.5.cloned.1.call-update) | async-done | bytes 1806352 | tf_op jit(solution)/shard_map/reduce_scatter | solution.py:82
  207.1 4.9 multiply_reduce_fusion.2
  215.4 51.2 %all-gather.7.cloned.1.call-done = bf16[4704,768]{1,0:T(8,128)(2,1)} async-done(((bf16[1176,768]{1,0:T(8,128)(2,1)}), bf16[4704,768]{1,0:T(8,128)(2,1)}) %all-gather.7.cloned.1.call-update) | async-done | bytes 7225360 | tf_op jit(solution)/shard_map/all_gather | solution.py:93
  266.6 11.9 %fusion.74 = f32[4704,768]{1,0:T(8,128)} fusion(bf16[4704,768]{1,0:T(8,128)(2,1)} %all-gather.7.cloned.1.call-done, bf16[768,768]{1,0:T(8,128)(2,1)} %param.25), kind=kOutput, calls=%fused_computation.132 | convolution fusion | flops 5549064192 | bytes 22855680 | tf_op jit(solution)/shard_map/dot_general | solution.py:94
  278.5 41.8 %all-gather.9.cloned.1.call-done = bf16[4704,768]{1,0:T(8,128)(2,1)} async-done(((bf16[1176,768]{1,0:T(8,128)(2,1)}), bf16[4704,768]{1,0:T(8,128)(2,1)}) %all-gather.9.cloned.1.call-update) | async-done | bytes 7225360 | tf_op jit(solution)/shard_map/all_gather | solution.py:110
  320.3 41.0 %fusion.68 = (f32[768]{0:T(1024)S(1)}, bf16[4704,768]{1,0:T(8,128)(2,1)}, f32[4704,768]{1,0:T(8,128)S(1)}) fusion(f32[4704,768]{1,0:T(8,128)} %fusion.74, f32[768]{0:T(1024)S(1)} %copy-done.50, bf16[4704,768]{1,0:T(8,128)(2,1)} %all-gather.9.cloned.1.call-done, bf16[768,768]{1,0:T(8,128)(2,1)S(1)} %copy-done), kind=kOutput, calls=%fused_computation.128 | convolution fusion | flops 5816400896 | bytes 44537856 | tf_op jit(solution)/shard_map/td,fd->tf/dot_general | solution.py:112
  361.3 4.3 multiply_convert_fusion.1
  365.6 10.8 %convolution_convert_fusion.1 = bf16[4704,768]{1,0:T(8,128)(2,1)} fusion(bf16[4704,768]{1,0:T(8,128)(2,1)} %multiply_convert_fusion.1, bf16[768,768]{1,0:T(8,128)(2,1)S(1)} %copy-done), kind=kOutput, calls=%fused_computation.25 | convolution fusion | flops 5552676864 | bytes 15630336 | tf_op jit(solution)/shard_map/dot_general | solution.py:99
  377.7 11.2 %convolution_convert_fusion = bf16[4704,768]{1,0:T(8,128)(2,1)} fusion(bf16[768,768]{1,0:T(8,128)(2,1)S(1)} %copy-done.54, bf16[4704,768]{1,0:T(8,128)(2,1)} %get-tuple-element.43), kind=kOutput, calls=%fused_computation.24 | convolution fusion | flops 5552676864 | bytes 15630336 | tf_op jit(solution)/shard_map/tf,df->td/dot_general | solution.py:120
  389.1 52.8 %reduce-scatter.7.cloned.1.call-done = bf16[1176,768]{1,0:T(8,128)(2,1)} async-done(((bf16[4704,768]{1,0:T(8,128)(2,1)}), bf16[1176,768]{1,0:T(8,128)(2,1)}) %reduce-scatter.7.cloned.1.call-update) | async-done | bytes 1806352 | tf_op jit(solution)/shard_map/reduce_scatter | solution.py:98
  441.8 67.6 %reduce-scatter.9.cloned.1.call-done = bf16[1176,768]{1,0:T(8,128)(2,1)} async-done(((bf16[4704,768]{1,0:T(8,128)(2,1)}), bf16[1176,768]{1,0:T(8,128)(2,1)}) %reduce-scatter.9.cloned.1.call-update) | async-done | bytes 1806352 | tf_op jit(solution)/shard_map/reduce_scatter | solution.py:119
  509.5 8.3 fusion.36
  523.5 51.8 %all-gather.11.cloned.1.call-done = bf16[4704,768]{1,0:T(8,128)(2,1)} async-done(((bf16[1176,768]{1,0:T(8,128)(2,1)}), bf16[4704,768]{1,0:T(8,128)(2,1)}) %all-gather.11.cloned.1.call-update) | async-done | bytes 7225360 | tf_op jit(solution)/shard_map/all_gather | solution.py:131
  575.3 6.8 convolution_convert_fusion.3
  582.1 6.2 reshape.193
  588.3 9.9 %convert_reduce_fusion.3 = (f32[3,64]{1,0:T(4,128)S(1)}, bf16[24,3,64,196]{3,2,1,0:T(8,128)(2,1)}) fusion(f32[24,3,196,196]{2,3,1,0:T(8,128)} %copy-done.2, f32[24,3,196]{2,1,0:T(4,128)S(1)} %copy-done.24, pred[24,196]{1,0:T(8,128)(4,1)S(1)} %copy-done.30, bf16[24,196,3,64]{1,0,3,2:T(8,128)(2,1)} %reshape.193), kind=kOutput, calls=%fused_computation.53 | convolution fusion | flops 367814976 | bytes 14738400 | tf_op jit(solution)/shard_map/ihqk,iqhd->ikhd/dot_general | solution.py:146
  599.8 11.2 %multiply_reduce_fusion = (f32[24,3,196]{2,1,0:T(4,128)S(1)}, f32[24,3,196,196]{2,3,1,0:T(8,128)}) fusion(f32[24,3,196,196]{2,3,1,0:T(8,128)S(1)} %bitcast.79, f32[24,3,196]{2,1,0:T(4,128)S(1)} %copy-done.24, pred[24,196]{1,0:T(8,128)(4,1)S(1)} %copy-done.30, f32[24,196,3,64]{1,0,3,2:T(8,128)} %squeeze.8, f32[3,64]{1,0:T(4,128)S(1)} %copy-done.47, ...), kind=kOutput, calls=%fused_computation.2 | convolution fusion | flops 369663840 | bytes 27664992 | tf_op jit(solution)/shard_map/iqhd,ikhd->ihqk/dot_general | solution.py:149
  611.0 10.2 %multiply_convert_fusion = bf16[24,3,196,196]{2,3,1,0:T(8,128)(2,1)} fusion(f32[24,3,196,196]{2,3,1,0:T(8,128)} %get-tuple-element.59, f32[24,3,196,196]{2,3,1,0:T(8,128)S(1)} %bitcast.79, f32[24,3,196]{2,1,0:T(4,128)S(1)} %get-tuple-element.58, f32[24,3,196]{2,1,0:T(4,128)S(1)} %copy-done.24, pred[24,196]{1,0:T(8,128)(4,1)S(1)} %copy-done.30), kind=kLoop, calls=%fused_computation.1 | loop fusion | flops 16595712 | bytes 27777120 | tf_op jit(solution)/shard_map/convert_element_type | solution.py:153
  621.2 8.7 fusion.43
  630.0 2.9 convert_reduce_fusion.4
  632.9 2.8 copy.53
  635.7 4.7 convert_element_type.185
  643.2 4.7 convert_element_type.179
  647.9 3.0 copy.50
  650.9 3.0 convert_element_type.182
  659.1 7.9 bitcast_convert_fusion
  667.1 11.8 %fusion.38 = f32[768,768]{1,0:T(8,128)} fusion(bf16[4704,768]{1,0:T(8,128)(2,1)} %all-gather.7.cloned.1.call-done, bf16[4704,768]{1,0:T(8,128)(2,1)} %get-tuple-element.43), kind=kOutput, calls=%fused_computation.78 | convolution fusion | flops 5549064192 | bytes 16809984 | tf_op jit(solution)/shard_map/td,tf->df/dot_general | solution.py:117
  678.9 12.2 %fusion.76 = f32[768,768]{1,0:T(8,128)} fusion(bf16[4704,768]{1,0:T(8,128)(2,1)} %multiply_convert_fusion.1, bf16[4704,768]{1,0:T(8,128)(2,1)} %all-gather.9.cloned.1.call-done), kind=kOutput, calls=%fused_computation.134 | convolution fusion | flops 5549064192 | bytes 16809984 | tf_op jit(solution)/shard_map/tf,td->fd/dot_general | solution.py:111
  693.6 5.9 fusion.8
  699.6 2.8 pad_maximum_fusion.1
  702.6 22.3 %all-reduce.1 = (f32[2,192]{1,0:T(2,128)}, f32[768]{0:T(1024)}) all-reduce(f32[2,192]{1,0:T(2,128)S(1)} %pad_maximum_fusion, f32[768]{0:T(1024)S(1)} %get-tuple-element.42), channel_id=1, replica_groups=mesh['dp'=8,'tensor'=4] {'dp'}, use_global_device_ids=true, to_apply=%region_22.23 | all-reduce | flops 1152 | bytes 9216 | tf_op jit(solution)/shard_map/psum | solution.py:205
  724.8 7.6 reduce-scatter.11.cloned.1.call-done
  732.4 3.4 fusion.37
  735.8 44.5 %all-reduce = (f32[768]{0:T(1024)}, f32[768]{0:T(1024)}, f32[768]{0:T(1024)}, f32[768]{0:T(1024)}, f32[768]{0:T(1024)}, /*index=5*/f32[768]{0:T(1024)}, f32[4]{0:T(128)S(1)}) all-reduce(f32[768]{0:T(1024)S(1)} %get-tuple-element.17, f32[768]{0:T(1024)S(1)} %get-tuple-element.25, ...), channel_id=1, replica_groups=mesh['dp'=8,'tensor'=4] {'dp','tensor'}, use_global_device_ids=true, to_apply=%region_16.17 | all-reduce | flops 4612 | bytes 36896 | tf_op jit(solution)/shard_map/psum | solution.py:193
  782.1 4.6 fusion.29
  786.7 183.9 %all-reduce.5.cloned.1.call-done = (f32[768,3,192]{0,2,1:T(8,128)}, f32[192,768]{1,0:T(8,128)}, f32[768,768]{1,0:T(8,128)}, f32[768,768]{1,0:T(8,128)}) async-done(((f32[768,3,192]{0,2,1:T(8,128)}, f32[192,768]{1,0:T(8,128)}, f32[768,768]{1,0:T(8,128)}, f32[768,768]{1,0:T(8,128)}), (f32[768,3,192]{0,2,1:T(8,128)}, f32[192,768]{1,0:T(8,128)}, f32[768,768]{1,0:T(8,128)}, ...) | async-done | bytes 7077904 | tf_op jit(solution)/shard_map/psum | solution.py:205
  970.6 2.9 copy.96
  (194 shorter events, 48.0 us)
Async XLA Ops:
  7.2 313.1 %copy-start = (bf16[768,768]{1,0:T(8,128)(2,1)S(1)}, bf16[768,768]{1,0:T(8,128)(2,1)}, u32[]{:S(2)}) copy-start(bf16[768,768]{1,0:T(8,128)(2,1)} %param.27) | copy-start | bytes 3538948
  7.2 8.9 copy-start.56
  7.2 62.0 %all-gather.5.cloned.1.call-start = ((), (), s32[]{:S(2)}) async-start(), calls=%async_computation.4 | async-start | bytes 9031680 | tf_op jit(solution)/shard_map/all_gather | solution.py:66
  14.7 189.8 %reduce-scatter.5.cloned.1.call-start = ((), (), s32[]{:S(2)}) async-start(), calls=%async_computation.5 | async-start | bytes 9031680 | tf_op jit(solution)/shard_map/reduce_scatter | solution.py:82
  16.8 97.2 %copy-start.29 = (pred[24,196]{1,0:T(8,128)(4,1)}, pred[24,196]{1,0:T(8,128)(4,1)S(1)}, u32[]{:S(2)}) copy-start(pred[24,196]{1,0:T(8,128)(4,1)S(1)} %get-tuple-element.54) | copy-start | bytes 14116
  114.0 11.1 %copy-start.23 = (f32[24,3,196]{2,1,0:T(4,128)}, f32[24,3,196]{2,1,0:T(4,128)S(1)}, u32[]{:S(2)}) copy-start(f32[24,3,196]{2,1,0:T(4,128)S(1)} %log_add_fusion) | copy-start | bytes 169348
  139.1 65.4 %copy-start.41 = (f32[768]{0:T(1024)S(1)}, f32[768]{0:T(1024)}, u32[]{:S(2)}) copy-start(f32[768]{0:T(1024)} %param.22) | copy-start | bytes 9220
  139.1 127.5 %all-gather.7.cloned.1.call-start = ((), (), s32[]{:S(2)}) async-start(), calls=%async_computation.6 | async-start | bytes 9031680 | tf_op jit(solution)/shard_map/all_gather | solution.py:93
  140.7 71.3 %copy-start.37 = (f32[1176]{0:T(1024)}, f32[1176]{0:T(1024)S(1)}, u32[]{:S(2)}) copy-start(f32[1176]{0:T(1024)S(1)} %get-tuple-element.46) | copy-start | bytes 14116
  140.7 71.9 %copy-start.44 = (f32[768]{0:T(1024)S(1)}, f32[768]{0:T(1024)}, u32[]{:S(2)}) copy-start(f32[768]{0:T(1024)} %param.23) | copy-start | bytes 9220
  140.7 71.9 %copy-start.52 = (f32[768]{0:T(1024)S(1)}, f32[768]{0:T(1024)}, u32[]{:S(2)}) copy-start(f32[768]{0:T(1024)} %param.24) | copy-start | bytes 9220
  214.8 105.5 %all-gather.9.cloned.1.call-start = ((), (), s32[]{:S(2)}) async-start(), calls=%async_computation.8 | async-start | bytes 9031680 | tf_op jit(solution)/shard_map/all_gather | solution.py:110
  215.4 104.9 %copy-start.50 = (f32[768]{0:T(1024)S(1)}, f32[768]{0:T(1024)}, u32[]{:S(2)}) copy-start(f32[768]{0:T(1024)} %param.26) | copy-start | bytes 9220
  215.4 226.5 %reduce-scatter.7.cloned.1.call-start = ((), (), s32[]{:S(2)}) async-start(), calls=%async_computation.7 | async-start | bytes 9031680 | tf_op jit(solution)/shard_map/reduce_scatter | solution.py:98
  320.3 41.1 %copy-start.13 = (f32[4704,768]{1,0:T(8,128)S(1)}, f32[4704,768]{1,0:T(8,128)}, u32[]{:S(2)}) copy-start(f32[4704,768]{1,0:T(8,128)} %fusion.74) | copy-start | bytes 43352068
  376.5 133.0 %reduce-scatter.9.cloned.1.call-start = ((), (), s32[]{:S(2)}) async-start(), calls=%async_computation.9 | async-start | bytes 9031680 | tf_op jit(solution)/shard_map/reduce_scatter | solution.py:119
  389.0 120.5 %copy-start.4 = (bf16[1176,768]{1,0:T(8,128)(2,1)S(1)}, bf16[1176,768]{1,0:T(8,128)(2,1)}, u32[]{:S(2)}) copy-start(bf16[1176,768]{1,0:T(8,128)(2,1)} %param.15) | copy-start | bytes 5419012
  389.0 120.5 %copy-start.34 = (f32[1176]{0:T(1024)S(1)}, f32[1176]{0:T(1024)}, u32[]{:S(2)}) copy-start(f32[1176]{0:T(1024)} %copy-done.33) | copy-start | bytes 14116
  389.0 120.5 %copy-start.38 = (f32[1176]{0:T(1024)S(1)}, f32[1176]{0:T(1024)}, u32[]{:S(2)}) copy-start(f32[1176]{0:T(1024)} %copy-done.37) | copy-start | bytes 14116
  389.0 120.5 %copy-start.40 = (f32[1176]{0:T(1024)S(1)}, f32[1176]{0:T(1024)}, u32[]{:S(2)}) copy-start(f32[1176]{0:T(1024)} %copy-done.39) | copy-start | bytes 14116
  389.0 120.5 %copy-start.42 = (f32[768]{0:T(1024)S(1)}, f32[768]{0:T(1024)}, u32[]{:S(2)}) copy-start(f32[768]{0:T(1024)} %param.22) | copy-start | bytes 9220
  389.0 120.5 %copy-start.45 = (f32[768]{0:T(1024)S(1)}, f32[768]{0:T(1024)}, u32[]{:S(2)}) copy-start(f32[768]{0:T(1024)} %param.23) | copy-start | bytes 9220
  389.0 120.5 %copy-start.51 = (f32[768]{0:T(1024)S(1)}, f32[768]{0:T(1024)}, u32[]{:S(2)}) copy-start(f32[768]{0:T(1024)} %param.28) | copy-start | bytes 9220
  389.0 186.2 %all-gather.11.cloned.1.call-start = ((), (), s32[]{:S(2)}) async-start(), calls=%async_computation.10 | async-start | bytes 9031680 | tf_op jit(solution)/shard_map/all_gather | solution.py:131
  520.2 55.1 %copy-start.28 = (bf16[192,768]{1,0:T(8,128)(2,1)S(1)}, bf16[192,768]{1,0:T(8,128)(2,1)}, u32[]{:S(2)}) copy-start(bf16[192,768]{1,0:T(8,128)(2,1)} %param.21) | copy-start | bytes 884740
  523.4 64.8 %copy-start.24 = (f32[24,3,196]{2,1,0:T(4,128)S(1)}, f32[24,3,196]{2,1,0:T(4,128)}, u32[]{:S(2)}) copy-start(f32[24,3,196]{2,1,0:T(4,128)} %copy-done.23) | copy-start | bytes 169348
  523.5 64.8 %copy-start.30 = (pred[24,196]{1,0:T(8,128)(4,1)S(1)}, pred[24,196]{1,0:T(8,128)(4,1)}, u32[]{:S(2)}) copy-start(pred[24,196]{1,0:T(8,128)(4,1)} %copy-done.29) | copy-start | bytes 14116
  523.5 208.9 %reduce-scatter.11.cloned.1.call-start = ((), (), s32[]{:S(2)}) async-start(), calls=%async_computation.11 | async-start | bytes 9031680 | tf_op jit(solution)/shard_map/reduce_scatter | solution.py:174
  582.1 16.2 %slice-start = ((s8[14745600]{0:T(1024)(128)(4,1)}), s8[2162688]{0:T(1024)(128)(4,1)S(1)}, s32[]{:S(2)}) async-start(s8[14745600]{0:T(1024)(128)(4,1)} %bitcast.78), calls=%async_computation.13 | async-start | bytes 4325376
  588.3 10.0 %slice-start.1 = ((s8[14745600]{0:T(1024)(128)(4,1)}), s8[4194304]{0:T(1024)(128)(4,1)S(1)}, s32[]{:S(2)}) async-start(s8[14745600]{0:T(1024)(128)(4,1)} %bitcast.78), calls=%async_computation.14 | async-start | bytes 8388608
  588.3 10.0 %slice-start.2 = ((s8[14745600]{0:T(1024)(128)(4,1)}), s8[4194304]{0:T(1024)(128)(4,1)S(1)}, s32[]{:S(2)}) async-start(s8[14745600]{0:T(1024)(128)(4,1)} %bitcast.78), calls=%async_computation.15 | async-start | bytes 8388608
  588.3 10.9 %slice-start.3 = ((s8[14745600]{0:T(1024)(128)(4,1)}), s8[4194304]{0:T(1024)(128)(4,1)S(1)}, s32[]{:S(2)}) async-start(s8[14745600]{0:T(1024)(128)(4,1)} %bitcast.78), calls=%async_computation.16 | async-start | bytes 8388608
  588.3 11.5 %copy-start.11 = (bf16[24,196,3,64]{1,0,3,2:T(8,128)(2,1)S(1)}, bf16[24,196,3,64]{1,0,3,2:T(8,128)(2,1)}, u32[]{:S(2)}) copy-start(bf16[24,196,3,64]{1,0,3,2:T(8,128)(2,1)} %reshape.193) | copy-start | bytes 5419012
  588.3 11.5 %copy-start.47 = (f32[3,64]{1,0:T(4,128)S(1)}, f32[3,64]{1,0:T(4,128)}, u32[]{:S(2)}) copy-start(f32[3,64]{1,0:T(4,128)} %add.138) | copy-start | bytes 2308
  611.0 10.2 %copy-start.48 = (f32[3,64]{1,0:T(4,128)S(1)}, f32[3,64]{1,0:T(4,128)}, u32[]{:S(2)}) copy-start(f32[3,64]{1,0:T(4,128)} %add.141) | copy-start | bytes 2308
  667.1 303.6 %all-reduce.5.cloned.1.call-start = ((), (), s32[]{:S(2)}) async-start(), calls=%async_computation.12 | async-start | bytes 14155776 | tf_op jit(solution)/shard_map/psum | solution.py:205
  667.1 24.0 %slice-start.8 = ((s8[7225344]{0:T(1024)(128)(4,1)}), s8[4194304]{0:T(1024)(128)(4,1)S(1)}, s32[]{:S(2)}) async-start(s8[7225344]{0:T(1024)(128)(4,1)} %bitcast.86), calls=%async_computation.21 | async-start | bytes 8388608
  667.1 26.5 %slice-start.4 = ((s8[5455872]{0:T(1024)(128)(4,1)}), s8[4194304]{0:T(1024)(128)(4,1)S(1)}, s32[]{:S(2)}) async-start(s8[5455872]{0:T(1024)(128)(4,1)} %bitcast.82), calls=%async_computation.17 | async-start | bytes 8388608
  667.1 26.5 %slice-start.6 = ((s8[7225344]{0:T(1024)(128)(4,1)}), s8[4194304]{0:T(1024)(128)(4,1)S(1)}, s32[]{:S(2)}) async-start(s8[7225344]{0:T(1024)(128)(4,1)} %bitcast.84), calls=%async_computation.19 | async-start | bytes 8388608
  678.9 12.2 %copy-start.14 = (bf16[4704,192]{0,1:T(8,128)(2,1)S(1)}, bf16[4704,192]{0,1:T(8,128)(2,1)}, u32[]{:S(2)}) copy-start(bf16[4704,192]{0,1:T(8,128)(2,1)} %convert_element_type.159) | copy-start | bytes 5419012
  678.9 12.2 %slice-start.9 = ((s8[7225344]{0:T(1024)(128)(4,1)}), s8[3031040]{0:T(1024)(128)(4,1)S(1)}, s32[]{:S(2)}) async-start(s8[7225344]{0:T(1024)(128)(4,1)} %bitcast.86), calls=%async_computation.22 | async-start | bytes 6062080
  678.9 14.7 %slice-start.5 = ((s8[5455872]{0:T(1024)(128)(4,1)}), s8[1261568]{0:T(1024)(128)(4,1)S(1)}, s32[]{:S(2)}) async-start(s8[5455872]{0:T(1024)(128)(4,1)} %bitcast.82), calls=%async_computation.18 | async-start | bytes 2523136
  678.9 14.7 %slice-start.7 = ((s8[7225344]{0:T(1024)(128)(4,1)}), s8[3031040]{0:T(1024)(128)(4,1)S(1)}, s32[]{:S(2)}) async-start(s8[7225344]{0:T(1024)(128)(4,1)} %bitcast.84), calls=%async_computation.20 | async-start | bytes 6062080
  699.5 32.8 %copy-start.5 = (bf16[1176,768]{1,0:T(8,128)(2,1)S(1)}, bf16[1176,768]{1,0:T(8,128)(2,1)}, u32[]{:S(2)}) copy-start(bf16[1176,768]{1,0:T(8,128)(2,1)} %param.15) | copy-start | bytes 5419012
  699.5 32.8 %copy-start.32 = (f32[1176]{0:T(1024)S(1)}, f32[1176]{0:T(1024)}, u32[]{:S(2)}) copy-start(f32[1176]{0:T(1024)} %copy-done.31) | copy-start | bytes 14116
  699.5 32.8 %copy-start.36 = (f32[1176]{0:T(1024)S(1)}, f32[1176]{0:T(1024)}, u32[]{:S(2)}) copy-start(f32[1176]{0:T(1024)} %copy-done.35) | copy-start | bytes 14116
  699.6 32.8 %copy-start.46 = (f32[768]{0:T(1024)S(1)}, f32[768]{0:T(1024)}, u32[]{:S(2)}) copy-start(f32[768]{0:T(1024)} %param.17) | copy-start | bytes 9220
  699.6 36.3 %copy-start.49 = (f32[768]{0:T(1024)S(1)}, f32[768]{0:T(1024)}, u32[]{:S(2)}) copy-start(f32[768]{0:T(1024)} %get-tuple-element.26) | copy-start | bytes 9220
  (28 other events, 124.3 us)
Sparse Core Ops, SparseCore 0:
  14.8 54.3 all-gather.4
  139.3 65.1 reduce-scatter.4
  214.9 51.6 all-gather.6
  268.6 51.6 all-gather.8
  376.6 65.1 reduce-scatter.6
  444.3 65.1 reduce-scatter.8
  523.6 51.6 all-gather.10
  667.2 65.1 reduce-scatter.10
  738.0 232.6 all-reduce.4
where the time goes:
time: 995 us; the launch traced here: 985 us
  waiting for transfers between devices  574 us (58%)
  matrix products  187 us (19%)
  local copies, waits for them, and re-layouts  81.1 us (8%)
  blocking collectives  66.7 us (7%)
  other arithmetic  61.1 us (6%)
  between operations  15.5 us (2%)
    psum x1, waiting for transfers between devices, on_device(): lax.psum((weight_qkv, grad_bias_qv, weight_out, weight_up, grad_bias_up,...  184 us
    reduce_scatter x1, waiting for transfers between devices, on_device(): lax.psum_scatter(jnp.einsum('tf,df->td', piece, w_up, preferred_element_t...  67.6 us
    reduce_scatter x1, waiting for transfers between devices, on_device(): lax.psum_scatter(jnp.dot(piece, w_out, preferred_element_type=jnp.float32...  63.8 us
    reduce_scatter x1, waiting for transfers between devices, on_device(): lax.psum_scatter(jnp.dot(piece, w_down, preferred_element_type=jnp.float3...  52.8 us
    all_gather x1, waiting for transfers between devices, on_device(): full_attn = lax.all_gather(in_attn, 'tensor', axis=0, tiled=True)  52.4 us
    all_gather x1, waiting for transfers between devices, on_device(): lax.all_gather(grad_hidden.astype(jnp.bfloat16), 'tensor', axis=0, tiled=...  51.8 us
    all_gather x1, waiting for transfers between devices, on_device(): full_mlp = lax.all_gather(in_mlp, 'tensor', axis=0, tiled=True)  51.2 us
    psum x1, blocking collectives, on_device(): lax.psum((grad_gain_attn, grad_shift_attn, grad_bias_out, grad_gain_mlp,...  44.5 us
  transfers between devices with their start and end apart: 9, of which 9 were waited for; matrix products, arithmetic and copies ran while one was open for 7% of the time, Pallas kernels for 0%

commit v1 on v0

--- a/solution.py
+++ b/solution.py
@@ -90,7 +90,18 @@
     hidden = inputs + branch
     normed_m, factor_m = normalize(hidden)
     in_mlp = (normed_m * gain_mlp + shift_mlp).astype(jnp.bfloat16)
-    full_mlp = lax.all_gather(in_mlp, "tensor", axis=0, tiled=True)
+    b_next = lax.psum(1, "tensor")
+    carry_in, t_next, low = (b_next, lax.axis_index("tensor"), in_mlp.shape[0])
+    inbox = []
+    for k0 in tuple(range(carry_in)):
+        inbox.append((k0, (k0 + 1) % carry_in))
+    full_mlp = jnp.zeros((*in_mlp.shape[:0], carry_in * low, *in_mlp.shape[1:]), in_mlp.dtype)
+    moved = in_mlp
+    for no in [*range(carry_in)]:
+        near = (t_next - no) % carry_in
+        full_mlp = lax.dynamic_update_slice_in_dim(full_mlp, moved, near * low, axis=0)
+        if no < carry_in - 1:
+            moved = lax.ppermute(moved, "tensor", inbox)
     pre_act = jnp.dot(full_mlp, w_up, preferred_element_type=jnp.float32) + bias_up
     act = exact_gelu(pre_act).astype(jnp.bfloat16)
     piece = act

time: 995 us -> 1020 us (1.025)
  starting transfers between devices: 0.37 us -> 12.1 us
  local copies, waits for them, and re-layouts: 81.1 us -> 92.3 us
    ppermute x0 -> x3, waiting for transfers between devices: none -> 93.2 us  [on_device(): moved = lax.ppermute(moved, 'tensor', inbox)]
    all_gather x1 -> x0, waiting for transfers between devices: 51.2 us -> none  [on_device(): full_mlp = lax.all_gather(in_mlp, 'tensor', axis=0, tiled=True)]
    all_gather x1, waiting for transfers between devices: 41.8 us -> 0.01 us  [on_device(): lax.all_gather(grad_stream.astype(jnp.bfloat16), 'tensor', axis=0, tiled=...]
    reduce_scatter x1, starting transfers between devices: 0.04 us -> 11.4 us  [on_device(): lax.psum_scatter(jnp.dot(piece, w_down, preferred_element_type=jnp.float3...]
    unnamed x140 -> x146, local copies, waits for them, and re-layouts: 20.2 us -> 23.8 us
  transfers between devices with their start and end apart: 9 -> 11, of which waited for: 9 -> 10; matrix products, arithmetic and copies ran while one was open for 7% -> 8% of each run, Pallas kernels for 0% -> 0%
where the time goes in v1:
time: 1020 us; the launch traced here: 1010 us
  waiting for transfers between devices  573 us (56%)
  matrix products  186 us (18%)
  local copies, waits for them, and re-layouts  92.3 us (9%)
  blocking collectives  66.7 us (7%)
  other arithmetic  59.6 us (6%)
  between operations  15.9 us (2%)
  starting transfers between devices  12.1 us (1%)
    psum x1, waiting for transfers between devices, on_device(): lax.psum((weight_qkv, grad_bias_qv, weight_out, weight_up, grad_bias_up,...  184 us
    ppermute x3, waiting for transfers between devices, on_device(): moved = lax.ppermute(moved, 'tensor', inbox)  93.2 us
    reduce_scatter x1, waiting for transfers between devices, on_device(): lax.psum_scatter(jnp.einsum('tf,df->td', piece, w_up, preferred_element_t...  67.6 us
    reduce_scatter x1, waiting for transfers between devices, on_device(): lax.psum_scatter(jnp.dot(piece, w_out, preferred_element_type=jnp.float32...  63.8 us
    reduce_scatter x1, waiting for transfers between devices, on_device(): lax.psum_scatter(jnp.dot(piece, w_down, preferred_element_type=jnp.float3...  53.1 us
    all_gather x1, waiting for transfers between devices, on_device(): full_attn = lax.all_gather(in_attn, 'tensor', axis=0, tiled=True)  52.4 us
    all_gather x1, waiting for transfers between devices, on_device(): lax.all_gather(grad_hidden.astype(jnp.bfloat16), 'tensor', axis=0, tiled=...  51.3 us
    psum x1, blocking collectives, on_device(): lax.psum((grad_gain_attn, grad_shift_attn, grad_bias_out, grad_gain_mlp,...  44.5 us
  transfers between devices with their start and end apart: 11, of which 10 were waited for; matrix products, arithmetic and copies ran while one was open for 8% of the time, Pallas kernels for 0%

profile of v1, /device:TPU:0, one launch (start us, length us, event | category | flops | bytes accessed | tf_op | source)
XLA Modules:
  0.0 1006.3 jit_solution(2038117565669979429)
XLA Ops:
  16.8 52.4 %all-gather.4.cloned.1.call-done = bf16[4704,768]{1,0:T(8,128)(2,1)} async-done(((bf16[1176,768]{1,0:T(8,128)(2,1)}), bf16[4704,768]{1,0:T(8,128)(2,1)}) %all-gather.4.cloned.1.call-update) | async-done | bytes 7225360 | tf_op jit(solution)/shard_map/all_gather | solution.py:66
  69.2 7.3 fusion.10
  77.9 3.5 fusion.73
  81.4 6.0 convert_element_type.155
  87.4 6.4 squeeze.9
  93.9 6.4 squeeze.8
  100.3 7.4 fusion.6
  108.3 4.5 exponential_reduce_fusion
  113.9 11.1 %convert_bitcast_fusion = bf16[24,196,3,64]{1,3,2,0:T(8,128)(2,1)S(1)} fusion(f32[24,196,3,64]{1,0,3,2:T(8,128)} %squeeze.8, f32[3,64]{1,0:T(4,128)} %add.166, f32[24,3,196,196]{2,3,1,0:T(8,128)} %copy-done.2, f32[24,3,196]{2,1,0:T(4,128)S(1)} %log_add_fusion, pred[24,196]{1,0:T(8,128)(4,1)S(1)} %get-tuple-element.56), kind=kOutput, calls=%fused_computation.91 | convolution fusion | flops 367815168 | bytes 16544736 | tf_op jit(solution)/shard_map/ihqk,ikhd->iqhd/dot_general | solution.py:76
  127.8 4.7 convert_element_type.159
  132.5 6.5 convolution_convert_fusion.2
  140.5 63.8 %reduce-scatter.5.cloned.1.call-done = bf16[1176,768]{1,0:T(8,128)(2,1)} async-done(((bf16[4704,768]{1,0:T(8,128)(2,1)}), bf16[1176,768]{1,0:T(8,128)(2,1)}) %reduce-scatter.5.cloned.1.call-update) | async-done | bytes 1806352 | tf_op jit(solution)/shard_map/reduce_scatter | solution.py:82
  206.9 4.7 multiply_reduce_fusion.2
  211.6 11.4 %reduce-scatter.7.cloned.1.call-start = ((), (), s32[]{:S(2)}) async-start(), calls=%async_computation.6 | async-start | bytes 9031680 | tf_op jit(solution)/shard_map/reduce_scatter | solution.py:109
  225.8 2.9 copy-done.21
  228.7 52.3 %collective-permute-done = bf16[1176,768]{1,0:T(8,128)(2,1)S(1)} collective-permute-done((bf16[1176,768]{1,0:T(8,128)(2,1)S(1)}, bf16[1176,768]{1,0:T(8,128)(2,1)S(1)}, u32[]{:S(2)}, u32[]{:S(2)}) %collective-permute-start) | collective-permute-done | bytes 1806368 | tf_op jit(solution)/shard_map/ppermute | solution.py:104
  281.1 22.4 %collective-permute-done.1 = bf16[1176,768]{1,0:T(8,128)(2,1)} collective-permute-done((bf16[1176,768]{1,0:T(8,128)(2,1)S(1)}, bf16[1176,768]{1,0:T(8,128)(2,1)}, u32[]{:S(2)}, u32[]{:S(2)}) %collective-permute-start.1) | collective-permute-done | bytes 1806368 | tf_op jit(solution)/shard_map/ppermute | solution.py:104
  307.7 18.4 %collective-permute-done.2 = bf16[1176,768]{1,0:T(8,128)(2,1)} collective-permute-done((bf16[1176,768]{1,0:T(8,128)(2,1)}, bf16[1176,768]{1,0:T(8,128)(2,1)}, u32[]{:S(2)}, u32[]{:S(2)}) %collective-permute-start.2) | collective-permute-done | bytes 1806368 | tf_op jit(solution)/shard_map/ppermute | solution.py:104
  329.0 11.6 %fusion.74 = f32[4704,768]{1,0:T(8,128)} fusion(bf16[4704,768]{1,0:T(8,128)(2,1)} %constant_dynamic-update-slice_fusion.3, bf16[768,768]{1,0:T(8,128)(2,1)S(1)} %copy-done.56), kind=kOutput, calls=%fused_computation.136 | convolution fusion | flops 5549064192 | bytes 22855680 | tf_op jit(solution)/shard_map/dot_general | solution.py:105
  340.7 41.1 %fusion.68 = (f32[768]{0:T(1024)S(1)}, bf16[4704,768]{1,0:T(8,128)(2,1)}, f32[4704,768]{1,0:T(8,128)S(1)}) fusion(f32[4704,768]{1,0:T(8,128)} %fusion.74, f32[768]{0:T(1024)S(1)} %copy-done.53, bf16[4704,768]{1,0:T(8,128)(2,1)} %all-gather.6.cloned.1.call-done, bf16[768,768]{1,0:T(8,128)(2,1)S(1)} %copy-done), kind=kOutput, calls=%fused_computation.132 | convolution fusion | flops 5816400896 | bytes 44537856 | tf_op jit(solution)/shard_map/td,fd->tf/dot_general | solution.py:123
  381.8 4.4 multiply_convert_fusion.1
  386.1 10.8 %convolution_convert_fusion.1 = bf16[4704,768]{1,0:T(8,128)(2,1)} fusion(bf16[4704,768]{1,0:T(8,128)(2,1)} %multiply_convert_fusion.1, bf16[768,768]{1,0:T(8,128)(2,1)S(1)} %copy-done), kind=kOutput, calls=%fused_computation.25 | convolution fusion | flops 5552676864 | bytes 15630336 | tf_op jit(solution)/shard_map/dot_general | solution.py:110
  398.2 10.8 %convolution_convert_fusion = bf16[4704,768]{1,0:T(8,128)(2,1)} fusion(bf16[768,768]{1,0:T(8,128)(2,1)S(1)} %copy-done.57, bf16[4704,768]{1,0:T(8,128)(2,1)} %get-tuple-element.43), kind=kOutput, calls=%fused_computation.24 | convolution fusion | flops 5552676864 | bytes 15630336 | tf_op jit(solution)/shard_map/tf,df->td/dot_general | solution.py:131
  409.2 53.1 %reduce-scatter.7.cloned.1.call-done = bf16[1176,768]{1,0:T(8,128)(2,1)} async-done(((bf16[4704,768]{1,0:T(8,128)(2,1)}), bf16[1176,768]{1,0:T(8,128)(2,1)}) %reduce-scatter.7.cloned.1.call-update) | async-done | bytes 1806352 | tf_op jit(solution)/shard_map/reduce_scatter | solution.py:109
  462.3 67.6 %reduce-scatter.9.cloned.1.call-done = bf16[1176,768]{1,0:T(8,128)(2,1)} async-done(((bf16[4704,768]{1,0:T(8,128)(2,1)}), bf16[1176,768]{1,0:T(8,128)(2,1)}) %reduce-scatter.9.cloned.1.call-update) | async-done | bytes 1806352 | tf_op jit(solution)/shard_map/reduce_scatter | solution.py:130
  530.0 8.3 fusion.36
  544.4 51.3 %all-gather.8.cloned.1.call-done = bf16[4704,768]{1,0:T(8,128)(2,1)} async-done(((bf16[1176,768]{1,0:T(8,128)(2,1)}), bf16[4704,768]{1,0:T(8,128)(2,1)}) %all-gather.8.cloned.1.call-update) | async-done | bytes 7225360 | tf_op jit(solution)/shard_map/all_gather | solution.py:142
  595.7 6.8 convolution_convert_fusion.3
  602.5 6.2 reshape.193
  608.7 9.9 convert_reduce_fusion.3
  620.3 11.3 %multiply_reduce_fusion = (f32[24,3,196]{2,1,0:T(4,128)S(1)}, f32[24,3,196,196]{2,3,1,0:T(8,128)}) fusion(f32[24,3,196,196]{2,3,1,0:T(8,128)S(1)} %bitcast.79, f32[24,3,196]{2,1,0:T(4,128)S(1)} %copy-done.26, pred[24,196]{1,0:T(8,128)(4,1)S(1)} %copy-done.32, f32[24,196,3,64]{1,0,3,2:T(8,128)} %squeeze.8, f32[3,64]{1,0:T(4,128)S(1)} %copy-done.49, ...), kind=kOutput, calls=%fused_computation.2 | convolution fusion | flops 369663840 | bytes 27664992 | tf_op jit(solution)/shard_map/iqhd,ikhd->ihqk/dot_general | solution.py:160
  631.5 10.2 %multiply_convert_fusion = bf16[24,3,196,196]{2,3,1,0:T(8,128)(2,1)} fusion(f32[24,3,196,196]{2,3,1,0:T(8,128)} %get-tuple-element.61, f32[24,3,196,196]{2,3,1,0:T(8,128)S(1)} %bitcast.79, f32[24,3,196]{2,1,0:T(4,128)S(1)} %get-tuple-element.60, f32[24,3,196]{2,1,0:T(4,128)S(1)} %copy-done.26, pred[24,196]{1,0:T(8,128)(4,1)S(1)} %copy-done.32), kind=kLoop, calls=%fused_computation.1 | loop fusion | flops 16595712 | bytes 27777120 | tf_op jit(solution)/shard_map/convert_element_type | solution.py:164
  641.8 8.7 fusion.43
  656.3 4.7 convert_element_type.185
  663.8 4.7 convert_element_type.179
  668.5 3.0 copy.50
  671.5 3.0 convert_element_type.182
  679.8 7.9 bitcast_convert_fusion
  687.8 11.8 %fusion.38 = f32[768,768]{1,0:T(8,128)} fusion(bf16[4704,768]{1,0:T(8,128)(2,1)} %constant_dynamic-update-slice_fusion.3, bf16[4704,768]{1,0:T(8,128)(2,1)} %get-tuple-element.43), kind=kOutput, calls=%fused_computation.78 | convolution fusion | flops 5549064192 | bytes 16809984 | tf_op jit(solution)/shard_map/td,tf->df/dot_general | solution.py:128
  699.6 12.2 %fusion.76 = f32[768,768]{1,0:T(8,128)} fusion(bf16[4704,768]{1,0:T(8,128)(2,1)} %multiply_convert_fusion.1, bf16[4704,768]{1,0:T(8,128)(2,1)} %all-gather.6.cloned.1.call-done), kind=kOutput, calls=%fused_computation.138 | convolution fusion | flops 5549064192 | bytes 16809984 | tf_op jit(solution)/shard_map/tf,td->fd/dot_general | solution.py:122
  714.3 5.9 fusion.8
  723.3 22.3 %all-reduce.1 = (f32[2,192]{1,0:T(2,128)}, f32[768]{0:T(1024)}) all-reduce(f32[2,192]{1,0:T(2,128)S(1)} %pad_maximum_fusion, f32[768]{0:T(1024)S(1)} %get-tuple-element.42), channel_id=1, replica_groups=mesh['dp'=8,'tensor'=4] {'dp'}, use_global_device_ids=true, to_apply=%region_22.23 | all-reduce | flops 1152 | bytes 9216 | tf_op jit(solution)/shard_map/psum | solution.py:216
  745.5 7.6 reduce-scatter.11.cloned.1.call-done
  753.1 3.4 fusion.37
  756.5 44.5 %all-reduce = (f32[768]{0:T(1024)}, f32[768]{0:T(1024)}, f32[768]{0:T(1024)}, f32[768]{0:T(1024)}, f32[768]{0:T(1024)}, /*index=5*/f32[768]{0:T(1024)}, f32[4]{0:T(128)S(1)}) all-reduce(f32[768]{0:T(1024)S(1)} %get-tuple-element.17, f32[768]{0:T(1024)S(1)} %get-tuple-element.25, ...), channel_id=1, replica_groups=mesh['dp'=8,'tensor'=4] {'dp','tensor'}, use_global_device_ids=true, to_apply=%region_16.17 | all-reduce | flops 4612 | bytes 36896 | tf_op jit(solution)/shard_map/psum | solution.py:204
  802.7 4.6 fusion.29
  807.4 183.9 %all-reduce.5.cloned.1.call-done = (f32[768,3,192]{0,2,1:T(8,128)}, f32[192,768]{1,0:T(8,128)}, f32[768,768]{1,0:T(8,128)}, f32[768,768]{1,0:T(8,128)}) async-done(((f32[768,3,192]{0,2,1:T(8,128)}, f32[192,768]{1,0:T(8,128)}, f32[768,768]{1,0:T(8,128)}, f32[768,768]{1,0:T(8,128)}), (f32[768,3,192]{0,2,1:T(8,128)}, f32[192,768]{1,0:T(8,128)}, f32[768,768]{1,0:T(8,128)}, ...) | async-done | bytes 7077904 | tf_op jit(solution)/shard_map/psum | solution.py:216
  991.3 2.9 copy.100
  (207 shorter events, 63.4 us)
Async XLA Ops:
  7.2 333.5 %copy-start = (bf16[768,768]{1,0:T(8,128)(2,1)S(1)}, bf16[768,768]{1,0:T(8,128)(2,1)}, u32[]{:S(2)}) copy-start(bf16[768,768]{1,0:T(8,128)(2,1)} %param.27) | copy-start | bytes 3538948
  7.2 62.0 %all-gather.4.cloned.1.call-start = ((), (), s32[]{:S(2)}) async-start(), calls=%async_computation.4 | async-start | bytes 9031680 | tf_op jit(solution)/shard_map/all_gather | solution.py:66
  14.7 189.7 %reduce-scatter.5.cloned.1.call-start = ((), (), s32[]{:S(2)}) async-start(), calls=%async_computation.5 | async-start | bytes 9031680 | tf_op jit(solution)/shard_map/reduce_scatter | solution.py:82
  16.8 97.1 %copy-start.31 = (pred[24,196]{1,0:T(8,128)(4,1)}, pred[24,196]{1,0:T(8,128)(4,1)S(1)}, u32[]{:S(2)}) copy-start(pred[24,196]{1,0:T(8,128)(4,1)S(1)} %get-tuple-element.56) | copy-start | bytes 14116
  113.9 11.1 %copy-start.25 = (f32[24,3,196]{2,1,0:T(4,128)}, f32[24,3,196]{2,1,0:T(4,128)S(1)}, u32[]{:S(2)}) copy-start(f32[24,3,196]{2,1,0:T(4,128)S(1)} %log_add_fusion) | copy-start | bytes 169348
  139.0 65.4 %copy-start.43 = (f32[768]{0:T(1024)S(1)}, f32[768]{0:T(1024)}, u32[]{:S(2)}) copy-start(f32[768]{0:T(1024)} %param.22) | copy-start | bytes 9220
  139.0 201.6 %all-gather.6.cloned.1.call-start = ((), (), s32[]{:S(2)}) async-start(), calls=%async_computation.7 | async-start | bytes 9031680 | tf_op jit(solution)/shard_map/all_gather | solution.py:121
  140.5 71.1 %copy-start.39 = (f32[1176]{0:T(1024)}, f32[1176]{0:T(1024)S(1)}, u32[]{:S(2)}) copy-start(f32[1176]{0:T(1024)S(1)} %get-tuple-element.46) | copy-start | bytes 14116
  206.7 16.9 %copy-start.35 = (f32[1176]{0:T(1024)}, f32[1176]{0:T(1024)S(1)}, u32[]{:S(2)}) copy-start(f32[1176]{0:T(1024)S(1)} %broadcast_multiply_fusion.4) | copy-start | bytes 14116
  211.6 12.0 %copy-start.46 = (f32[768]{0:T(1024)S(1)}, f32[768]{0:T(1024)}, u32[]{:S(2)}) copy-start(f32[768]{0:T(1024)} %param.23) | copy-start | bytes 9220
  211.6 12.0 %copy-start.52 = (f32[768]{0:T(1024)S(1)}, f32[768]{0:T(1024)}, u32[]{:S(2)}) copy-start(f32[768]{0:T(1024)} %param.24) | copy-start | bytes 9220
  211.6 250.6 %reduce-scatter.7.cloned.1.call-start = ((), (), s32[]{:S(2)}) async-start(), calls=%async_computation.6 | async-start | bytes 9031680 | tf_op jit(solution)/shard_map/reduce_scatter | solution.py:109
  228.7 52.3 %collective-permute-start = (bf16[1176,768]{1,0:T(8,128)(2,1)S(1)}, bf16[1176,768]{1,0:T(8,128)(2,1)S(1)}, u32[]{:S(2)}, u32[]{:S(2)}) collective-permute-start(bf16[1176,768]{1,0:T(8,128)(2,1)S(1)} %get-tuple-element.50), channel_id=1, source_target_pairs={{0,1},{1,2},{2,3},{3,0},{4,5},{5,6},{6,7},{7,4},{8,9},{9,10},{10,1... | collective-permute-start | bytes 5419016 | tf_op jit(solution)/shard_map/ppermute | solution.py:104
  281.1 22.4 %collective-permute-start.1 = (bf16[1176,768]{1,0:T(8,128)(2,1)S(1)}, bf16[1176,768]{1,0:T(8,128)(2,1)}, u32[]{:S(2)}, u32[]{:S(2)}) collective-permute-start(bf16[1176,768]{1,0:T(8,128)(2,1)S(1)} %collective-permute-done), channel_id=1, source_target_pairs={{0,1},{1,2},{2,3},{3,0},{4,5},{5,6},{6,7},{7,4},{8,9},{9,10},{10,1... | collective-permute-start | bytes 5419016 | tf_op jit(solution)/shard_map/ppermute | solution.py:104
  303.5 22.7 %collective-permute-start.2 = (bf16[1176,768]{1,0:T(8,128)(2,1)}, bf16[1176,768]{1,0:T(8,128)(2,1)}, u32[]{:S(2)}, u32[]{:S(2)}) collective-permute-start(bf16[1176,768]{1,0:T(8,128)(2,1)} %collective-permute-done.1), channel_id=1, source_target_pairs={{0,1},{1,2},{2,3},{3,0},{4,5},{5,6},{6,7},{7,4},{8,9},{9,10},{10,1... | collective-permute-start | bytes 5419016 | tf_op jit(solution)/shard_map/ppermute | solution.py:104
  303.5 25.5 %copy-start.56 = (bf16[768,768]{1,0:T(8,128)(2,1)S(1)}, bf16[768,768]{1,0:T(8,128)(2,1)}, u32[]{:S(2)}) copy-start(bf16[768,768]{1,0:T(8,128)(2,1)} %param.25) | copy-start | bytes 3538948
  329.0 11.6 %copy-start.53 = (f32[768]{0:T(1024)S(1)}, f32[768]{0:T(1024)}, u32[]{:S(2)}) copy-start(f32[768]{0:T(1024)} %param.26) | copy-start | bytes 9220
  340.7 41.1 %copy-start.14 = (f32[4704,768]{1,0:T(8,128)S(1)}, f32[4704,768]{1,0:T(8,128)}, u32[]{:S(2)}) copy-start(f32[4704,768]{1,0:T(8,128)} %fusion.74) | copy-start | bytes 43352068
  397.0 133.0 %reduce-scatter.9.cloned.1.call-start = ((), (), s32[]{:S(2)}) async-start(), calls=%async_computation.8 | async-start | bytes 9031680 | tf_op jit(solution)/shard_map/reduce_scatter | solution.py:130
  409.0 120.9 %copy-start.4 = (bf16[1176,768]{1,0:T(8,128)(2,1)S(1)}, bf16[1176,768]{1,0:T(8,128)(2,1)}, u32[]{:S(2)}) copy-start(bf16[1176,768]{1,0:T(8,128)(2,1)} %param.15) | copy-start | bytes 5419012
  409.0 120.9 %copy-start.36 = (f32[1176]{0:T(1024)S(1)}, f32[1176]{0:T(1024)}, u32[]{:S(2)}) copy-start(f32[1176]{0:T(1024)} %copy-done.35) | copy-start | bytes 14116
  409.0 120.9 %copy-start.40 = (f32[1176]{0:T(1024)S(1)}, f32[1176]{0:T(1024)}, u32[]{:S(2)}) copy-start(f32[1176]{0:T(1024)} %copy-done.39) | copy-start | bytes 14116
  409.0 120.9 %copy-start.42 = (f32[1176]{0:T(1024)S(1)}, f32[1176]{0:T(1024)}, u32[]{:S(2)}) copy-start(f32[1176]{0:T(1024)} %copy-done.41) | copy-start | bytes 14116
  409.0 120.9 %copy-start.44 = (f32[768]{0:T(1024)S(1)}, f32[768]{0:T(1024)}, u32[]{:S(2)}) copy-start(f32[768]{0:T(1024)} %param.22) | copy-start | bytes 9220
  409.1 120.9 %copy-start.47 = (f32[768]{0:T(1024)S(1)}, f32[768]{0:T(1024)}, u32[]{:S(2)}) copy-start(f32[768]{0:T(1024)} %param.23) | copy-start | bytes 9220
  409.1 120.9 %copy-start.54 = (f32[768]{0:T(1024)S(1)}, f32[768]{0:T(1024)}, u32[]{:S(2)}) copy-start(f32[768]{0:T(1024)} %param.28) | copy-start | bytes 9220
  409.1 186.6 %all-gather.8.cloned.1.call-start = ((), (), s32[]{:S(2)}) async-start(), calls=%async_computation.9 | async-start | bytes 9031680 | tf_op jit(solution)/shard_map/all_gather | solution.py:142
  540.7 55.0 %copy-start.30 = (bf16[192,768]{1,0:T(8,128)(2,1)S(1)}, bf16[192,768]{1,0:T(8,128)(2,1)}, u32[]{:S(2)}) copy-start(bf16[192,768]{1,0:T(8,128)(2,1)} %param.21) | copy-start | bytes 884740
  543.9 64.8 %copy-start.26 = (f32[24,3,196]{2,1,0:T(4,128)S(1)}, f32[24,3,196]{2,1,0:T(4,128)}, u32[]{:S(2)}) copy-start(f32[24,3,196]{2,1,0:T(4,128)} %copy-done.25) | copy-start | bytes 169348
  543.9 64.8 %copy-start.32 = (pred[24,196]{1,0:T(8,128)(4,1)S(1)}, pred[24,196]{1,0:T(8,128)(4,1)}, u32[]{:S(2)}) copy-start(pred[24,196]{1,0:T(8,128)(4,1)} %copy-done.31) | copy-start | bytes 14116
  543.9 209.2 %reduce-scatter.11.cloned.1.call-start = ((), (), s32[]{:S(2)}) async-start(), calls=%async_computation.10 | async-start | bytes 9031680 | tf_op jit(solution)/shard_map/reduce_scatter | solution.py:185
  602.5 16.2 %slice-start = ((s8[14745600]{0:T(1024)(128)(4,1)}), s8[2162688]{0:T(1024)(128)(4,1)S(1)}, s32[]{:S(2)}) async-start(s8[14745600]{0:T(1024)(128)(4,1)} %bitcast.78), calls=%async_computation.12 | async-start | bytes 4325376
  608.7 10.9 %slice-start.3 = ((s8[14745600]{0:T(1024)(128)(4,1)}), s8[4194304]{0:T(1024)(128)(4,1)S(1)}, s32[]{:S(2)}) async-start(s8[14745600]{0:T(1024)(128)(4,1)} %bitcast.78), calls=%async_computation.15 | async-start | bytes 8388608
  608.7 11.5 %copy-start.12 = (bf16[24,196,3,64]{1,0,3,2:T(8,128)(2,1)S(1)}, bf16[24,196,3,64]{1,0,3,2:T(8,128)(2,1)}, u32[]{:S(2)}) copy-start(bf16[24,196,3,64]{1,0,3,2:T(8,128)(2,1)} %reshape.193) | copy-start | bytes 5419012
  608.7 11.5 %copy-start.49 = (f32[3,64]{1,0:T(4,128)S(1)}, f32[3,64]{1,0:T(4,128)}, u32[]{:S(2)}) copy-start(f32[3,64]{1,0:T(4,128)} %add.166) | copy-start | bytes 2308
  687.7 303.5 %all-reduce.5.cloned.1.call-start = ((), (), s32[]{:S(2)}) async-start(), calls=%async_computation.11 | async-start | bytes 14155776 | tf_op jit(solution)/shard_map/psum | solution.py:216
  687.8 24.0 %slice-start.8 = ((s8[7225344]{0:T(1024)(128)(4,1)}), s8[4194304]{0:T(1024)(128)(4,1)S(1)}, s32[]{:S(2)}) async-start(s8[7225344]{0:T(1024)(128)(4,1)} %bitcast.86), calls=%async_computation.20 | async-start | bytes 8388608
  687.8 26.5 %slice-start.4 = ((s8[5455872]{0:T(1024)(128)(4,1)}), s8[4194304]{0:T(1024)(128)(4,1)S(1)}, s32[]{:S(2)}) async-start(s8[5455872]{0:T(1024)(128)(4,1)} %bitcast.82), calls=%async_computation.16 | async-start | bytes 8388608
  687.8 26.5 %slice-start.6 = ((s8[7225344]{0:T(1024)(128)(4,1)}), s8[4194304]{0:T(1024)(128)(4,1)S(1)}, s32[]{:S(2)}) async-start(s8[7225344]{0:T(1024)(128)(4,1)} %bitcast.84), calls=%async_computation.18 | async-start | bytes 8388608
  699.6 12.2 %copy-start.15 = (bf16[4704,192]{0,1:T(8,128)(2,1)S(1)}, bf16[4704,192]{0,1:T(8,128)(2,1)}, u32[]{:S(2)}) copy-start(bf16[4704,192]{0,1:T(8,128)(2,1)} %convert_element_type.159) | copy-start | bytes 5419012
  699.6 12.2 %slice-start.9 = ((s8[7225344]{0:T(1024)(128)(4,1)}), s8[3031040]{0:T(1024)(128)(4,1)S(1)}, s32[]{:S(2)}) async-start(s8[7225344]{0:T(1024)(128)(4,1)} %bitcast.86), calls=%async_computation.21 | async-start | bytes 6062080
  699.6 14.7 %slice-start.5 = ((s8[5455872]{0:T(1024)(128)(4,1)}), s8[1261568]{0:T(1024)(128)(4,1)S(1)}, s32[]{:S(2)}) async-start(s8[5455872]{0:T(1024)(128)(4,1)} %bitcast.82), calls=%async_computation.17 | async-start | bytes 2523136
  699.6 14.7 %slice-start.7 = ((s8[7225344]{0:T(1024)(128)(4,1)}), s8[3031040]{0:T(1024)(128)(4,1)S(1)}, s32[]{:S(2)}) async-start(s8[7225344]{0:T(1024)(128)(4,1)} %bitcast.84), calls=%async_computation.19 | async-start | bytes 6062080
  720.2 32.8 %copy-start.5 = (bf16[1176,768]{1,0:T(8,128)(2,1)S(1)}, bf16[1176,768]{1,0:T(8,128)(2,1)}, u32[]{:S(2)}) copy-start(bf16[1176,768]{1,0:T(8,128)(2,1)} %param.15) | copy-start | bytes 5419012
  720.2 32.8 %copy-start.34 = (f32[1176]{0:T(1024)S(1)}, f32[1176]{0:T(1024)}, u32[]{:S(2)}) copy-start(f32[1176]{0:T(1024)} %copy-done.33) | copy-start | bytes 14116
  720.2 32.8 %copy-start.38 = (f32[1176]{0:T(1024)S(1)}, f32[1176]{0:T(1024)}, u32[]{:S(2)}) copy-start(f32[1176]{0:T(1024)} %copy-done.37) | copy-start | bytes 14116
  720.2 32.8 %copy-start.48 = (f32[768]{0:T(1024)S(1)}, f32[768]{0:T(1024)}, u32[]{:S(2)}) copy-start(f32[768]{0:T(1024)} %param.17) | copy-start | bytes 9220
  720.3 36.2 %copy-start.51 = (f32[768]{0:T(1024)S(1)}, f32[768]{0:T(1024)}, u32[]{:S(2)}) copy-start(f32[768]{0:T(1024)} %get-tuple-element.26) | copy-start | bytes 9220
  (33 other events, 164.9 us)
Sparse Core Ops, SparseCore 0:
  14.8 54.3 all-gather.3
  139.1 65.1 reduce-scatter.4
  211.8 66.7 all-gather.5
  397.1 65.1 reduce-scatter.6
  464.7 65.1 reduce-scatter.8
  544.0 51.6 all-gather.7
  687.9 65.1 reduce-scatter.10
  758.6 232.5 all-reduce.4
